TPU v7x, 512 devices: a whole 4x4x16 slice. The times are simulated.
512 devices in a mesh: pipe: 8 (over y, core), seq: 64 (over x, z).
Axes of the slice: x: 4, y: 4, z: 16, core: 2. Of those that a mesh axis runs over, the one named last changes fastest.
Arguments:
- inputs: bfloat16 [2, 32768, 512], P(None, 'seq'), may hold values from -6 to 6
- w_in: bfloat16 [8, 512, 2048], P('pipe'), may hold values from -0.25 to 0.25
- w_out: bfloat16 [8, 512, 512], P('pipe'), may hold values from -0.25 to 0.25
- lengths: int32 [2, 16], replicated, may hold values from 1 to 8192, 32768 in all within a row
- valid: int32 [2, 64], replicated, may hold values from 128 to 512
Outputs:
- states: bfloat16 [8, 2, 32768, 512], P('pipe', None, 'seq')
Inputs may be any that keep to these rules, and one draw needn't show every extreme that they name: Each row of stream lengths sums to 32768.
All inputs are finite; a program needn't handle non-finite values.
Results may differ from a plain program's by a relative error of at most 0.025.
Values may be sent and summed in bfloat16 or wider, within the bound.
A program may use at most 64 MiB of HBM per device.

v0:
```python
import math

import jax
import jax.numpy as jnp
from jax import lax
from jax.sharding import PartitionSpec as P

HEAD_DIM = 128
WINDOW = 512


norm_eps = 1e-05
out_eps = 0.001


def shifted(x, axis, by):
    size = lax.axis_size(axis)
    pairs = [(i, i + by) for i in range(size) if 0 <= i + by < size]
    return lax.ppermute(x, axis, pairs)


def layer_norm(values, epsilon):
    mean = jnp.mean(values, axis=-1, keepdims=True)
    centred = values - mean
    spread = jnp.mean(centred * centred, axis=-1, keepdims=True)
    return centred * lax.rsqrt(spread + epsilon)


def shards(inputs, w_in, w_out, lengths, valid):
    micro = inputs.shape[0]
    tok = inputs.shape[1]
    width = inputs.shape[2]
    branch_width = w_out.shape[1]
    heads = branch_width // HEAD_DIM
    groups = valid.shape[1]
    sections = lax.axis_size("pipe")
    section = lax.axis_index("pipe")
    block_index = lax.axis_index("seq")
    key_rows = WINDOW + tok
    wide_in = w_in[0]
    wide_out = w_out[0]
    kv_weight = jnp.concatenate(
        [wide_in[:, 3 * branch_width :], wide_in[:, branch_width : 2 * branch_width]], 1
    )
    score_scale = 1.0 / math.sqrt(HEAD_DIM)
    mix_scale = 1.0 / math.sqrt(WINDOW)
    key_pos = block_index * tok - WINDOW + jnp.arange(key_rows, dtype=jnp.int32)
    query_pos = key_pos[WINDOW:]
    key_block = jnp.floor_divide(key_pos, tok)
    group_ids = jnp.arange(groups, dtype=jnp.int32)

    def project(x_rows):
        normed = layer_norm(x_rows.astype(jnp.float32), norm_eps).astype(jnp.bfloat16)
        proj = jax.nn.silu(jnp.dot(normed, wide_in, preferred_element_type=jnp.float32)).astype(
            jnp.bfloat16
        )
        return (normed, proj)

    def project_spare(x_rows):
        return (
            jnp.zeros((tok, width), jnp.bfloat16),
            jnp.zeros((tok, 4 * branch_width), jnp.bfloat16),
        )

    def tick(step, carry):
        incoming, states = carry
        slot = step - section
        active = (slot >= 0) & (slot < micro)
        index = jnp.clip(slot, 0, micro - 1)
        fresh = lax.dynamic_index_in_dim(inputs, index, 0, keepdims=False)
        x_rows = jnp.where(section == 0, fresh, incoming)
        bounds = jnp.cumsum(lax.dynamic_index_in_dim(lengths, index, 0, keepdims=False))
        valid_row = lax.dynamic_index_in_dim(valid, index, 0, keepdims=False)
        counts = jnp.sum(
            jnp.where(key_block[:, None] == group_ids[None, :], valid_row[None, :], 0), axis=1
        )
        key_live = (key_pos >= 0) & (jnp.mod(key_pos, tok) < counts)
        key_stream = jnp.sum((key_pos[:, None] >= bounds[None, :]).astype(jnp.int32), axis=1)
        query_live = key_live[WINDOW:]
        query_stream = key_stream[WINDOW:]
        allowed = (
            query_live[:, None]
            & key_live[None, :]
            & (query_stream[:, None] == key_stream[None, :])
            & (key_pos[None, :] <= query_pos[:, None])
            & (query_pos[:, None] - key_pos[None, :] < WINDOW)
        )
        normed, proj = lax.cond(active, project, project_spare, x_rows)
        own_kv = jnp.concatenate(
            [proj[:, 3 * branch_width :], proj[:, branch_width : 2 * branch_width]], 1
        )
        pieces = [shifted(normed, "seq", 1)]
        received = jnp.concatenate(pieces, 0)

        def finish(x_rows):
            remote_kv = jax.nn.silu(
                jnp.dot(received, kv_weight, preferred_element_type=jnp.float32)
            ).astype(jnp.bfloat16)
            all_kv = jnp.concatenate([remote_kv, own_kv], 0)
            keys = all_kv[:, :branch_width].reshape(key_rows, heads, HEAD_DIM)
            values = all_kv[:, branch_width:].reshape(key_rows, heads, HEAD_DIM)
            query = proj[:, 2 * branch_width : 3 * branch_width].reshape(tok, heads, HEAD_DIM)
            scores = jnp.einsum("qhd,khd->hqk", query, keys, preferred_element_type=jnp.float32)
            weights = jnp.where(
                allowed[None], jax.nn.silu(scores * score_scale) * mix_scale, 0.0
            ).astype(jnp.bfloat16)
            attended = jnp.einsum(
                "hqk,khd->qhd", weights, values, preferred_element_type=jnp.float32
            ).reshape(tok, branch_width)
            gated = (
                layer_norm(attended, out_eps) * proj[:, :branch_width].astype(jnp.float32)
            ).astype(jnp.bfloat16)
            return (
                x_rows.astype(jnp.float32)
                + jnp.dot(gated, wide_out, preferred_element_type=jnp.float32)
            ).astype(jnp.bfloat16)

        def finish_spare(x_rows):
            return x_rows

        result = lax.cond(active, finish, finish_spare, x_rows)
        zero_index = jnp.zeros((), jnp.int32)
        updated = lax.dynamic_update_slice(
            states, result[None, None], (zero_index, index, zero_index, zero_index)
        )
        states = jnp.where(active, updated, states)
        incoming = shifted(result, "pipe", 1)
        return (incoming, states)

    start_states = jnp.zeros((1, micro, tok, width), jnp.bfloat16)
    start_rows = jnp.zeros((tok, width), jnp.bfloat16)
    final_rows, states = lax.fori_loop(0, sections + micro - 1, tick, (start_rows, start_states))
    return states


def solution(mesh):
    in_specs = (P(None, "seq", None), P("pipe", None, None), P("pipe", None, None), P(), P())
    out_specs = P("pipe", None, "seq", None)
    return jax.shard_map(shards, mesh=mesh, in_specs=in_specs, out_specs=out_specs, check_vma=False)
```

profile of v0, /device:TPU:31, one launch (start us, length us, event | category | flops | bytes accessed | tf_op | source)
XLA Modules:
  0.0 408.7 jit_solution(4944272313689636705)
XLA Ops:
  3.5 405.2 %while.20 = (s32[]{:T(128)}, bf16[512,512]{1,0:T(8,128)(2,1)S(1)}, bf16[1,2,512,512]{3,2,1,0:T(8,128)(2,1)}, s32[]{:T(128)}, pred[]{:T(512)}, /*index=5*/bf16[2,...) while((s32[]{:T(128)}, bf16[512,512]{1,0:T(8,128)(2,1)S(1)}, ...), condition=%wide.region_12.13_spmd.clone.clone, body=%wide.region_0.12_spmd.clone.clone.sunk | while | flops 2994503936 | bytes 57458204 | solution.py:132
  5.7 3.5 collective-permute-start
  12.7 16.4 %collective-permute-done = bf16[512,512]{1,0:T(8,128)(2,1)} collective-permute-done((bf16[512,512]{1,0:T(8,128)(2,1)}, bf16[512,512]{1,0:T(8,128)(2,1)}, u32[]{:S(2)}, u32[]{:S(2)}) %collective-permute-start) | collective-permute-done | bytes 524320 | tf_op jit(solution)/shard_map/while/body/eval_jaxpr/ppermute | solution.py:19
  41.2 7.0 %collective-permute-done = bf16[512,512]{1,0:T(8,128)(2,1)} collective-permute-done((bf16[512,512]{1,0:T(8,128)(2,1)}, bf16[512,512]{1,0:T(8,128)(2,1)}, u32[]{:S(2)}, u32[]{:S(2)}) %collective-permute-start) | collective-permute-done | bytes 524320 | tf_op jit(solution)/shard_map/while/body/eval_jaxpr/ppermute | solution.py:19
  51.6 8.4 %collective-permute-done.1 = bf16[512,512]{1,0:T(8,128)(2,1)S(1)} collective-permute-done((bf16[512,512]{1,0:T(8,128)(2,1)S(1)}, bf16[512,512]{1,0:T(8,128)(2,1)S(1)}, u32[]{:S(2)}, u32[]{:S(2)}) %collective-permute-start.1) | collective-permute-done | bytes 524320 | tf_op jit(solution)/shard_map/while/body/eval_jaxpr/ppermute | solution.py:19
  67.5 7.0 %collective-permute-done = bf16[512,512]{1,0:T(8,128)(2,1)} collective-permute-done((bf16[512,512]{1,0:T(8,128)(2,1)}, bf16[512,512]{1,0:T(8,128)(2,1)}, u32[]{:S(2)}, u32[]{:S(2)}) %collective-permute-start) | collective-permute-done | bytes 524320 | tf_op jit(solution)/shard_map/while/body/eval_jaxpr/ppermute | solution.py:19
  77.8 8.6 %collective-permute-done.1 = bf16[512,512]{1,0:T(8,128)(2,1)S(1)} collective-permute-done((bf16[512,512]{1,0:T(8,128)(2,1)S(1)}, bf16[512,512]{1,0:T(8,128)(2,1)S(1)}, u32[]{:S(2)}, u32[]{:S(2)}) %collective-permute-start.1) | collective-permute-done | bytes 524320 | tf_op jit(solution)/shard_map/while/body/eval_jaxpr/ppermute | solution.py:19
  94.0 7.0 %collective-permute-done = bf16[512,512]{1,0:T(8,128)(2,1)} collective-permute-done((bf16[512,512]{1,0:T(8,128)(2,1)}, bf16[512,512]{1,0:T(8,128)(2,1)}, u32[]{:S(2)}, u32[]{:S(2)}) %collective-permute-start) | collective-permute-done | bytes 524320 | tf_op jit(solution)/shard_map/while/body/eval_jaxpr/ppermute | solution.py:19
  104.3 8.4 %collective-permute-done.1 = bf16[512,512]{1,0:T(8,128)(2,1)S(1)} collective-permute-done((bf16[512,512]{1,0:T(8,128)(2,1)S(1)}, bf16[512,512]{1,0:T(8,128)(2,1)S(1)}, u32[]{:S(2)}, u32[]{:S(2)}) %collective-permute-start.1) | collective-permute-done | bytes 524320 | tf_op jit(solution)/shard_map/while/body/eval_jaxpr/ppermute | solution.py:19
  120.2 7.0 %collective-permute-done = bf16[512,512]{1,0:T(8,128)(2,1)} collective-permute-done((bf16[512,512]{1,0:T(8,128)(2,1)}, bf16[512,512]{1,0:T(8,128)(2,1)}, u32[]{:S(2)}, u32[]{:S(2)}) %collective-permute-start) | collective-permute-done | bytes 524320 | tf_op jit(solution)/shard_map/while/body/eval_jaxpr/ppermute | solution.py:19
  130.6 8.4 %collective-permute-done.1 = bf16[512,512]{1,0:T(8,128)(2,1)S(1)} collective-permute-done((bf16[512,512]{1,0:T(8,128)(2,1)S(1)}, bf16[512,512]{1,0:T(8,128)(2,1)S(1)}, u32[]{:S(2)}, u32[]{:S(2)}) %collective-permute-start.1) | collective-permute-done | bytes 524320 | tf_op jit(solution)/shard_map/while/body/eval_jaxpr/ppermute | solution.py:19
  146.5 7.0 %collective-permute-done = bf16[512,512]{1,0:T(8,128)(2,1)} collective-permute-done((bf16[512,512]{1,0:T(8,128)(2,1)}, bf16[512,512]{1,0:T(8,128)(2,1)}, u32[]{:S(2)}, u32[]{:S(2)}) %collective-permute-start) | collective-permute-done | bytes 524320 | tf_op jit(solution)/shard_map/while/body/eval_jaxpr/ppermute | solution.py:19
  156.9 8.4 %collective-permute-done.1 = bf16[512,512]{1,0:T(8,128)(2,1)S(1)} collective-permute-done((bf16[512,512]{1,0:T(8,128)(2,1)S(1)}, bf16[512,512]{1,0:T(8,128)(2,1)S(1)}, u32[]{:S(2)}, u32[]{:S(2)}) %collective-permute-start.1) | collective-permute-done | bytes 524320 | tf_op jit(solution)/shard_map/while/body/eval_jaxpr/ppermute | solution.py:19
  172.8 7.0 %collective-permute-done = bf16[512,512]{1,0:T(8,128)(2,1)} collective-permute-done((bf16[512,512]{1,0:T(8,128)(2,1)}, bf16[512,512]{1,0:T(8,128)(2,1)}, u32[]{:S(2)}, u32[]{:S(2)}) %collective-permute-start) | collective-permute-done | bytes 524320 | tf_op jit(solution)/shard_map/while/body/eval_jaxpr/ppermute | solution.py:19
  183.1 133.0 %collective-permute-done.1 = bf16[512,512]{1,0:T(8,128)(2,1)S(1)} collective-permute-done((bf16[512,512]{1,0:T(8,128)(2,1)S(1)}, bf16[512,512]{1,0:T(8,128)(2,1)S(1)}, u32[]{:S(2)}, u32[]{:S(2)}) %collective-permute-start.1) | collective-permute-done | bytes 524320 | tf_op jit(solution)/shard_map/while/body/eval_jaxpr/ppermute | solution.py:19
  317.3 4.3 %conditional.8 = (bf16[512,512]{1,0:T(8,128)(2,1)}, bf16[512,2048]{1,0:T(8,128)(2,1)S(1)}) conditional(s32[]{:T(128)} %convert_element_type.103, () %tuple.141, (bf16[512,512]{1,0:T(8,128)(2,1)S(1)}, bf16[512,2048]{1,0:T(8,128)(2,1)}) %tuple.142), branch_computations={%region_1.1_spmd, %region_2.4_spmd} | conditional | flops 1081606656 | bytes 15222828 | solution.py:88
  318.9 2.7 multiply_convert_fusion
  326.9 7.0 %collective-permute-done = bf16[512,512]{1,0:T(8,128)(2,1)} collective-permute-done((bf16[512,512]{1,0:T(8,128)(2,1)}, bf16[512,512]{1,0:T(8,128)(2,1)}, u32[]{:S(2)}, u32[]{:S(2)}) %collective-permute-start) | collective-permute-done | bytes 524320 | tf_op jit(solution)/shard_map/while/body/eval_jaxpr/ppermute | solution.py:19
  334.0 18.5 %conditional.9 = (bf16[512,512]{1,0:T(8,128)(2,1)S(1)}) conditional(s32[]{:T(128)} %convert_element_type.103, bf16[512,512]{1,0:T(8,128)(2,1)S(1)} %bitcast_select_fusion.3, (bf16[512,512]{1,0:T(8,128)(2,1)S(1)}, bf16[512,512]{1,0:T(8,128)(2,1)}, bf16[512,1024]{1,0:T(8,128)(2,1)}, bf16[512,1024]{1,0:T(8,128)(2,1)}, s32[1024]{0:T(1024)S(1)}, ...), branch_computations={%region_6.6_spmd, %region_7.11_spmd.clone.clone} | conditional | flops 1910228480 | bytes 30599768 | solution.py:121
  335.4 2.4 multiply_convert_fusion.1
  339.4 2.3 copy.28
  341.7 2.5 copy.27
  345.3 5.2 %fusion.52 = (f32[512]{0:T(512)S(1)}, f32[4,128,512]{2,1,0:T(8,128)S(1)}) fusion(bf16[1024,4,128]{0,2,1:T(8,128)(2,1)} %bitcast.82, pred[512,1024]{0,1:T(8,128)(4,1)S(1)} %fusion.24, bf16[512,4,128]{0,2,1:T(8,128)(2,1)S(1)} %bitcast.83, bf16[128,4,8,128]{3,2,1,0:T(8,128)(2,1)} %get-tuple-element.1018), kind=kOutput, calls=%fused_computation.81 | convolution fusion | flops 1090780672 | bytes 4196352 | tf_op jit(solution)/shard_map/while/body/eval_jaxpr/cond/branch_1_fun/hqk,khd->qhd/dot_general | solution.py:107
  355.8 11.3 %collective-permute-done.1 = bf16[512,512]{1,0:T(8,128)(2,1)S(1)} collective-permute-done((bf16[512,512]{1,0:T(8,128)(2,1)S(1)}, bf16[512,512]{1,0:T(8,128)(2,1)S(1)}, u32[]{:S(2)}, u32[]{:S(2)}) %collective-permute-start.1) | collective-permute-done | bytes 524320 | tf_op jit(solution)/shard_map/while/body/eval_jaxpr/ppermute | solution.py:19
  368.2 4.3 %conditional.8 = (bf16[512,512]{1,0:T(8,128)(2,1)}, bf16[512,2048]{1,0:T(8,128)(2,1)S(1)}) conditional(s32[]{:T(128)} %convert_element_type.103, () %tuple.141, (bf16[512,512]{1,0:T(8,128)(2,1)S(1)}, bf16[512,2048]{1,0:T(8,128)(2,1)}) %tuple.142), branch_computations={%region_1.1_spmd, %region_2.4_spmd} | conditional | flops 1081606656 | bytes 15222828 | solution.py:88
  369.8 2.7 multiply_convert_fusion
  377.9 8.5 %collective-permute-done = bf16[512,512]{1,0:T(8,128)(2,1)} collective-permute-done((bf16[512,512]{1,0:T(8,128)(2,1)}, bf16[512,512]{1,0:T(8,128)(2,1)}, u32[]{:S(2)}, u32[]{:S(2)}) %collective-permute-start) | collective-permute-done | bytes 524320 | tf_op jit(solution)/shard_map/while/body/eval_jaxpr/ppermute | solution.py:19
  386.4 18.5 %conditional.9 = (bf16[512,512]{1,0:T(8,128)(2,1)S(1)}) conditional(s32[]{:T(128)} %convert_element_type.103, bf16[512,512]{1,0:T(8,128)(2,1)S(1)} %bitcast_select_fusion.3, (bf16[512,512]{1,0:T(8,128)(2,1)S(1)}, bf16[512,512]{1,0:T(8,128)(2,1)}, bf16[512,1024]{1,0:T(8,128)(2,1)}, bf16[512,1024]{1,0:T(8,128)(2,1)}, s32[1024]{0:T(1024)S(1)}, ...), branch_computations={%region_6.6_spmd, %region_7.11_spmd.clone.clone} | conditional | flops 1910228480 | bytes 30599768 | solution.py:121
  387.8 2.4 multiply_convert_fusion.1
  391.9 2.3 copy.28
  394.1 2.5 copy.27
  397.7 5.2 %fusion.52 = (f32[512]{0:T(512)S(1)}, f32[4,128,512]{2,1,0:T(8,128)S(1)}) fusion(bf16[1024,4,128]{0,2,1:T(8,128)(2,1)} %bitcast.82, pred[512,1024]{0,1:T(8,128)(4,1)S(1)} %fusion.24, bf16[512,4,128]{0,2,1:T(8,128)(2,1)S(1)} %bitcast.83, bf16[128,4,8,128]{3,2,1,0:T(8,128)(2,1)} %get-tuple-element.1018), kind=kOutput, calls=%fused_computation.81 | convolution fusion | flops 1090780672 | bytes 4196352 | tf_op jit(solution)/shard_map/while/body/eval_jaxpr/cond/branch_1_fun/hqk,khd->qhd/dot_general | solution.py:107
  (255 shorter events, 121.0 us)
Async XLA Ops:
  1.3 2.2 copy-start.3
  1.3 2.2 copy-start.4
  5.7 23.3 %collective-permute-start = (bf16[512,512]{1,0:T(8,128)(2,1)}, bf16[512,512]{1,0:T(8,128)(2,1)}, u32[]{:S(2)}, u32[]{:S(2)}) collective-permute-start(bf16[512,512]{1,0:T(8,128)(2,1)} %get-tuple-element.1117), channel_id=1, source_target_pairs={{0,1},{1,2},{2,3},{3,4},{4,5},{5,6},{6,7},{7,8},{8,9},{9,10},{10,1... | collective-permute-start | bytes 1572872 | tf_op jit(solution)/shard_map/while/body/eval_jaxpr/ppermute | solution.py:19
  29.1 4.6 %collective-permute-start.1 = (bf16[512,512]{1,0:T(8,128)(2,1)S(1)}, bf16[512,512]{1,0:T(8,128)(2,1)S(1)}, u32[]{:S(2)}, u32[]{:S(2)}) collective-permute-start(bf16[512,512]{1,0:T(8,128)(2,1)S(1)} %get-tuple-element.1180), channel_id=1, source_target_pairs={{0,64},{64,128},{128,192},{192,256},{256,320},{320,384},{384,448},... | collective-permute-start | bytes 1572872 | tf_op jit(solution)/shard_map/while/body/eval_jaxpr/ppermute | solution.py:19
  35.9 12.4 %collective-permute-start = (bf16[512,512]{1,0:T(8,128)(2,1)}, bf16[512,512]{1,0:T(8,128)(2,1)}, u32[]{:S(2)}, u32[]{:S(2)}) collective-permute-start(bf16[512,512]{1,0:T(8,128)(2,1)} %get-tuple-element.1117), channel_id=1, source_target_pairs={{0,1},{1,2},{2,3},{3,4},{4,5},{5,6},{6,7},{7,8},{8,9},{9,10},{10,1... | collective-permute-start | bytes 1572872 | tf_op jit(solution)/shard_map/while/body/eval_jaxpr/ppermute | solution.py:19
  48.3 11.6 %collective-permute-start.1 = (bf16[512,512]{1,0:T(8,128)(2,1)S(1)}, bf16[512,512]{1,0:T(8,128)(2,1)S(1)}, u32[]{:S(2)}, u32[]{:S(2)}) collective-permute-start(bf16[512,512]{1,0:T(8,128)(2,1)S(1)} %get-tuple-element.1180), channel_id=1, source_target_pairs={{0,64},{64,128},{128,192},{192,256},{256,320},{320,384},{384,448},... | collective-permute-start | bytes 1572872 | tf_op jit(solution)/shard_map/while/body/eval_jaxpr/ppermute | solution.py:19
  62.1 12.4 %collective-permute-start = (bf16[512,512]{1,0:T(8,128)(2,1)}, bf16[512,512]{1,0:T(8,128)(2,1)}, u32[]{:S(2)}, u32[]{:S(2)}) collective-permute-start(bf16[512,512]{1,0:T(8,128)(2,1)} %get-tuple-element.1117), channel_id=1, source_target_pairs={{0,1},{1,2},{2,3},{3,4},{4,5},{5,6},{6,7},{7,8},{8,9},{9,10},{10,1... | collective-permute-start | bytes 1572872 | tf_op jit(solution)/shard_map/while/body/eval_jaxpr/ppermute | solution.py:19
  74.5 11.9 %collective-permute-start.1 = (bf16[512,512]{1,0:T(8,128)(2,1)S(1)}, bf16[512,512]{1,0:T(8,128)(2,1)S(1)}, u32[]{:S(2)}, u32[]{:S(2)}) collective-permute-start(bf16[512,512]{1,0:T(8,128)(2,1)S(1)} %get-tuple-element.1180), channel_id=1, source_target_pairs={{0,64},{64,128},{128,192},{192,256},{256,320},{320,384},{384,448},... | collective-permute-start | bytes 1572872 | tf_op jit(solution)/shard_map/while/body/eval_jaxpr/ppermute | solution.py:19
  88.7 12.4 %collective-permute-start = (bf16[512,512]{1,0:T(8,128)(2,1)}, bf16[512,512]{1,0:T(8,128)(2,1)}, u32[]{:S(2)}, u32[]{:S(2)}) collective-permute-start(bf16[512,512]{1,0:T(8,128)(2,1)} %get-tuple-element.1117), channel_id=1, source_target_pairs={{0,1},{1,2},{2,3},{3,4},{4,5},{5,6},{6,7},{7,8},{8,9},{9,10},{10,1... | collective-permute-start | bytes 1572872 | tf_op jit(solution)/shard_map/while/body/eval_jaxpr/ppermute | solution.py:19
  101.0 11.6 %collective-permute-start.1 = (bf16[512,512]{1,0:T(8,128)(2,1)S(1)}, bf16[512,512]{1,0:T(8,128)(2,1)S(1)}, u32[]{:S(2)}, u32[]{:S(2)}) collective-permute-start(bf16[512,512]{1,0:T(8,128)(2,1)S(1)} %get-tuple-element.1180), channel_id=1, source_target_pairs={{0,64},{64,128},{128,192},{192,256},{256,320},{320,384},{384,448},... | collective-permute-start | bytes 1572872 | tf_op jit(solution)/shard_map/while/body/eval_jaxpr/ppermute | solution.py:19
  114.9 12.4 %collective-permute-start = (bf16[512,512]{1,0:T(8,128)(2,1)}, bf16[512,512]{1,0:T(8,128)(2,1)}, u32[]{:S(2)}, u32[]{:S(2)}) collective-permute-start(bf16[512,512]{1,0:T(8,128)(2,1)} %get-tuple-element.1117), channel_id=1, source_target_pairs={{0,1},{1,2},{2,3},{3,4},{4,5},{5,6},{6,7},{7,8},{8,9},{9,10},{10,1... | collective-permute-start | bytes 1572872 | tf_op jit(solution)/shard_map/while/body/eval_jaxpr/ppermute | solution.py:19
  127.3 11.6 %collective-permute-start.1 = (bf16[512,512]{1,0:T(8,128)(2,1)S(1)}, bf16[512,512]{1,0:T(8,128)(2,1)S(1)}, u32[]{:S(2)}, u32[]{:S(2)}) collective-permute-start(bf16[512,512]{1,0:T(8,128)(2,1)S(1)} %get-tuple-element.1180), channel_id=1, source_target_pairs={{0,64},{64,128},{128,192},{192,256},{256,320},{320,384},{384,448},... | collective-permute-start | bytes 1572872 | tf_op jit(solution)/shard_map/while/body/eval_jaxpr/ppermute | solution.py:19
  141.2 12.4 %collective-permute-start = (bf16[512,512]{1,0:T(8,128)(2,1)}, bf16[512,512]{1,0:T(8,128)(2,1)}, u32[]{:S(2)}, u32[]{:S(2)}) collective-permute-start(bf16[512,512]{1,0:T(8,128)(2,1)} %get-tuple-element.1117), channel_id=1, source_target_pairs={{0,1},{1,2},{2,3},{3,4},{4,5},{5,6},{6,7},{7,8},{8,9},{9,10},{10,1... | collective-permute-start | bytes 1572872 | tf_op jit(solution)/shard_map/while/body/eval_jaxpr/ppermute | solution.py:19
  153.6 11.6 %collective-permute-start.1 = (bf16[512,512]{1,0:T(8,128)(2,1)S(1)}, bf16[512,512]{1,0:T(8,128)(2,1)S(1)}, u32[]{:S(2)}, u32[]{:S(2)}) collective-permute-start(bf16[512,512]{1,0:T(8,128)(2,1)S(1)} %get-tuple-element.1180), channel_id=1, source_target_pairs={{0,64},{64,128},{128,192},{192,256},{256,320},{320,384},{384,448},... | collective-permute-start | bytes 1572872 | tf_op jit(solution)/shard_map/while/body/eval_jaxpr/ppermute | solution.py:19
  167.4 12.4 %collective-permute-start = (bf16[512,512]{1,0:T(8,128)(2,1)}, bf16[512,512]{1,0:T(8,128)(2,1)}, u32[]{:S(2)}, u32[]{:S(2)}) collective-permute-start(bf16[512,512]{1,0:T(8,128)(2,1)} %get-tuple-element.1117), channel_id=1, source_target_pairs={{0,1},{1,2},{2,3},{3,4},{4,5},{5,6},{6,7},{7,8},{8,9},{9,10},{10,1... | collective-permute-start | bytes 1572872 | tf_op jit(solution)/shard_map/while/body/eval_jaxpr/ppermute | solution.py:19
  179.8 136.3 %collective-permute-start.1 = (bf16[512,512]{1,0:T(8,128)(2,1)S(1)}, bf16[512,512]{1,0:T(8,128)(2,1)S(1)}, u32[]{:S(2)}, u32[]{:S(2)}) collective-permute-start(bf16[512,512]{1,0:T(8,128)(2,1)S(1)} %get-tuple-element.1180), channel_id=1, source_target_pairs={{0,64},{64,128},{128,192},{192,256},{256,320},{320,384},{384,448},... | collective-permute-start | bytes 1572872 | tf_op jit(solution)/shard_map/while/body/eval_jaxpr/ppermute | solution.py:19
  317.3 1.6 copy-start.1
  321.6 12.4 %collective-permute-start = (bf16[512,512]{1,0:T(8,128)(2,1)}, bf16[512,512]{1,0:T(8,128)(2,1)}, u32[]{:S(2)}, u32[]{:S(2)}) collective-permute-start(bf16[512,512]{1,0:T(8,128)(2,1)} %get-tuple-element.1117), channel_id=1, source_target_pairs={{0,1},{1,2},{2,3},{3,4},{4,5},{5,6},{6,7},{7,8},{8,9},{9,10},{10,1... | collective-permute-start | bytes 1572872 | tf_op jit(solution)/shard_map/while/body/eval_jaxpr/ppermute | solution.py:19
  335.4 2.4 copy-start
  350.5 1.5 copy-start.2
  352.5 14.6 %collective-permute-start.1 = (bf16[512,512]{1,0:T(8,128)(2,1)S(1)}, bf16[512,512]{1,0:T(8,128)(2,1)S(1)}, u32[]{:S(2)}, u32[]{:S(2)}) collective-permute-start(bf16[512,512]{1,0:T(8,128)(2,1)S(1)} %get-tuple-element.1180), channel_id=1, source_target_pairs={{0,64},{64,128},{128,192},{192,256},{256,320},{320,384},{384,448},... | collective-permute-start | bytes 1572872 | tf_op jit(solution)/shard_map/while/body/eval_jaxpr/ppermute | solution.py:19
  368.2 1.6 copy-start.1
  372.5 13.8 %collective-permute-start = (bf16[512,512]{1,0:T(8,128)(2,1)}, bf16[512,512]{1,0:T(8,128)(2,1)}, u32[]{:S(2)}, u32[]{:S(2)}) collective-permute-start(bf16[512,512]{1,0:T(8,128)(2,1)} %get-tuple-element.1117), channel_id=1, source_target_pairs={{0,1},{1,2},{2,3},{3,4},{4,5},{5,6},{6,7},{7,8},{8,9},{9,10},{10,1... | collective-permute-start | bytes 1572872 | tf_op jit(solution)/shard_map/while/body/eval_jaxpr/ppermute | solution.py:19
  387.8 2.4 copy-start
  402.9 1.5 copy-start.2
  404.9 3.8 collective-permute-start.1
where the time goes:
time: 411 us; the launch traced here: 409 us
  waiting for transfers between devices  262 us (64%)
  other arithmetic  62 us (15%)
  local copies, waits for them, and re-layouts  30.9 us (8%)
  starting transfers between devices  30.5 us (7%)
  matrix products  21.7 us (5%)
    ppermute x18, waiting for transfers between devices, shifted(): return lax.ppermute(x, axis, pairs)  262 us
    ppermute x18, starting transfers between devices, shifted(): return lax.ppermute(x, axis, pairs)  30.5 us
    concatenate x9, other arithmetic, tick(): jnp.concatenate([proj[:, 3 * branch_width:], proj[:, branch_width:2 * bra...  19.2 us
    select_n x9, other arithmetic, tick(): states = jnp.where(active, updated, states)  17.8 us
    another operation x53, local copies, waits for them, and re-layouts  13.5 us
    dot_general x2, matrix products, finish(): jnp.einsum('hqk,khd->qhd', weights, values, preferred_element_type=jnp.fl...  10.4 us
    select_n x9, other arithmetic, tick(): x_rows = jnp.where(section == 0, fresh, incoming)  9.88 us
  transfers between devices with their start and end apart: 18, of which 18 were waited for; matrix products, arithmetic and copies ran while one was open for 12% of the time, Pallas kernels for 0%

commit v1 on v0

v1 whole, which is shorter than its diff:
```python
import functools
import math

import jax
import jax.numpy as jnp
from jax import lax
from jax.experimental import pallas as pl
from jax.experimental.pallas import tpu as pltpu
from jax.sharding import PartitionSpec as P

MESH = pl.DeviceIdType.MESH

HEAD_DIM = 128
WINDOW = 512
CH = 128
BF = jnp.bfloat16
F32 = jnp.float32

norm_eps = 1e-05
out_eps = 0.001


def half_silu(h):
    h = h.astype(BF)
    return h + h * jnp.tanh(h)


def kernel(micro, tok, width, hd, sections, blocks, streams,
           inp, win, wout, lens, valid, out,
           xin, hn, nb, w1, w2, qb, ub, kb, vb, mask,
           ld_sem, xs, xr, hs, hr):
    p = lax.axis_index("pipe")
    b = lax.axis_index("seq")
    heads = hd // HEAD_DIM
    span = WINDOW + CH
    n_ch = tok // CH
    right = lax.rem(b + 1, blocks)
    left = lax.rem(b + blocks - 1, blocks)
    up = lax.rem(p + 1, sections)
    down = lax.rem(p + sections - 1, sections)

    barrier = pltpu.get_barrier_semaphore()
    for dev in ((p, left), (p, right), (up, b), (down, b)):
        pl.semaphore_signal(barrier, inc=1, device_id=dev, device_id_type=MESH)

    load_in = pltpu.make_async_copy(win.at[0], w1, ld_sem.at[0])
    load_out = pltpu.make_async_copy(wout.at[0], w2, ld_sem.at[1])
    load_x = pltpu.make_async_copy(inp, xin, ld_sem.at[2])

    @pl.when(p == 0)
    def _():
        load_x.start()

    load_in.start()
    load_out.start()

    score_scale = 0.5 / math.sqrt(HEAD_DIM)
    ii = lax.broadcasted_iota(jnp.int32, (CH, 1), 0)
    jj = lax.broadcasted_iota(jnp.int32, (1, span), 1)

    def make_mask(step, carry):
        m = step // n_ch
        k = lax.rem(step, n_ch)
        row = k * CH + ii
        col = k * CH + jj - WINDOW
        q_pos = b * tok + row
        k_pos = b * tok + col
        q_stream = jnp.zeros_like(q_pos)
        k_stream = jnp.zeros_like(k_pos)
        bound = jnp.int32(0)
        for n in range(streams):
            bound = bound + lens[m, n]
            q_stream = q_stream + jnp.where(q_pos >= bound, 1, 0)
            k_stream = k_stream + jnp.where(k_pos >= bound, 1, 0)
        here = valid[m, b]
        before = valid[m, left]
        k_count = jnp.where(col >= 0, here, before)
        k_row = jnp.where(col >= 0, col, col + tok)
        k_code = jnp.where((k_row < k_count) & (k_pos >= 0), k_stream, -1)
        q_code = jnp.where(row < here, q_stream, -2)
        ok = (q_code == k_code) & (jj > ii) & (jj <= ii + WINDOW)
        mask[m, k] = jnp.where(ok, score_scale, 0.0)
        return carry

    lax.fori_loop(0, micro * n_ch, make_mask, 0)

    pl.semaphore_wait(barrier, 4)

    @pl.when(p == 0)
    def _():
        load_x.wait()

    load_in.wait()
    load_out.wait()

    def x_copy(m, k):
        rows = pl.ds(pl.multiple_of(k * CH, CH), CH)
        return pltpu.make_async_remote_copy(
            src_ref=out.at[0, m, rows], dst_ref=xin.at[m, rows],
            send_sem=xs.at[m, k], recv_sem=xr.at[m, k],
            device_id=(up, b), device_id_type=MESH)

    def h_copy(m, k):
        rows = pl.ds(pl.multiple_of(k * CH, CH), CH)
        return pltpu.make_async_remote_copy(
            src_ref=nb.at[m, rows], dst_ref=hn.at[m, rows],
            send_sem=hs.at[m, k], recv_sem=hr.at[m, k],
            device_id=(p, right), device_id_type=MESH)

    def own(m, step):
        k = n_ch - 1 - step
        base = pl.multiple_of(k * CH, CH)
        rows = pl.ds(base, CH)

        @pl.when(p > 0)
        def _():
            x_copy(m, k).wait_recv()

        x = xin[m, rows].astype(F32)
        mean = jnp.mean(x, axis=-1, keepdims=True)
        cen = x - mean
        var = jnp.mean(cen * cen, axis=-1, keepdims=True)
        nrm = (cen * (0.5 * lax.rsqrt(var + norm_eps))).astype(BF)
        nb[m, rows] = nrm
        h_copy(m, k).start()
        own_rows = pl.ds(pl.multiple_of(WINDOW + base, CH), CH)
        for ref, at, rr in ((ub, 0, rows), (vb, 1, own_rows), (qb, 2, rows), (kb, 3, own_rows)):
            ref[rr] = half_silu(jnp.dot(
                nrm, w1[:, at * hd:(at + 1) * hd], preferred_element_type=F32))

    def attend(m, step):
        k = n_ch - 1 - step
        base = pl.multiple_of(k * CH, CH)
        rows = pl.ds(base, CH)
        h_copy(m, k).wait_recv()
        nrm = hn[m, rows]
        for ref, at in ((kb, 3), (vb, 1)):
            ref[rows] = half_silu(jnp.dot(
                nrm, w1[:, at * hd:(at + 1) * hd], preferred_element_type=F32))
        keys = pl.ds(base, span)
        mk = mask[m, k]
        parts = []
        for h in range(heads):
            cols = slice(h * HEAD_DIM, (h + 1) * HEAD_DIM)
            s = lax.dot_general(qb[rows, cols], kb[keys, cols], (((1,), (1,)), ((), ())),
                                preferred_element_type=F32)
            a = half_silu(s * mk)
            parts.append(jnp.dot(a, vb[keys, cols], preferred_element_type=F32))
        att = jnp.concatenate(parts, 1)
        mean = jnp.mean(att, axis=-1, keepdims=True)
        cen = att - mean
        var = jnp.mean(cen * cen, axis=-1, keepdims=True)
        gated = (cen * lax.rsqrt(var + out_eps * WINDOW) * ub[rows].astype(F32)).astype(BF)
        res = xin[m, rows].astype(F32) + jnp.dot(gated, w2[...], preferred_element_type=F32)
        out[0, m, rows] = res.astype(BF)

        @pl.when(p < sections - 1)
        def _():
            x_copy(m, k).start()

    for m in range(micro):
        def own_step(step, carry, m=m):
            own(m, step)
            return carry

        def att_step(step, carry, m=m):
            attend(m, step)
            return carry

        lax.fori_loop(0, n_ch, own_step, 0)
        lax.fori_loop(0, n_ch, att_step, 0)

    for m in range(micro):
        for k in range(n_ch):
            h_copy(m, k).wait_send()

            @pl.when(p < sections - 1)
            def _():
                x_copy(m, k).wait_send()


def shards(mesh, inputs, w_in, w_out, lengths, valid):
    micro, tok, width = inputs.shape
    hd = w_out.shape[1]
    sections = mesh.shape["pipe"]
    blocks = mesh.shape["seq"]
    streams = lengths.shape[1]
    n_ch = tok // CH
    hbm = pl.BlockSpec(memory_space=pl.ANY)
    smem = pl.BlockSpec(memory_space=pltpu.SMEM)
    return pl.pallas_call(
        functools.partial(kernel, micro, tok, width, hd, sections, blocks, streams),
        out_shape=jax.ShapeDtypeStruct((1, micro, tok, width), BF),
        in_specs=[hbm, hbm, hbm, smem, smem],
        out_specs=pl.BlockSpec(memory_space=pltpu.VMEM),
        scratch_shapes=[
            pltpu.VMEM((micro, tok, width), BF),
            pltpu.VMEM((micro, tok, width), BF),
            pltpu.VMEM((micro, tok, width), BF),
            pltpu.VMEM((width, 4 * hd), BF),
            pltpu.VMEM((hd, width), BF),
            pltpu.VMEM((tok, hd), BF),
            pltpu.VMEM((tok, hd), BF),
            pltpu.VMEM((WINDOW + tok, hd), BF),
            pltpu.VMEM((WINDOW + tok, hd), BF),
            pltpu.VMEM((micro, n_ch, CH, WINDOW + CH), F32),
            pltpu.SemaphoreType.DMA((3,)),
            pltpu.SemaphoreType.DMA((micro, n_ch)),
            pltpu.SemaphoreType.DMA((micro, n_ch)),
            pltpu.SemaphoreType.DMA((micro, n_ch)),
            pltpu.SemaphoreType.DMA((micro, n_ch)),
        ],
        compiler_params=pltpu.CompilerParams(
            collective_id=0, has_side_effects=True, vmem_limit_bytes=48 << 20),
    )(inputs, w_in, w_out, lengths, valid)


def solution(mesh):
    in_specs = (P(None, "seq", None), P("pipe", None, None), P("pipe", None, None), P(), P())
    out_specs = P("pipe", None, "seq", None)
    return jax.shard_map(functools.partial(shards, mesh), mesh=mesh, in_specs=in_specs,
                         out_specs=out_specs, check_vma=False)
```

time: 411 us -> 104 us (0.25)
  the two profiles are of different devices: /device:TPU:31 before, /device:TPU:25 now
where the time goes in v1:
time: 104 us
  Pallas kernels  97.7 us (94%)
  local copies, waits for them, and re-layouts  6.19 us (6%)
    pallas_call x1, Pallas kernels, shards(): pl.pallas_call(functools.partial(kernel, micro, tok, width, hd, sections,...  97.7 us
    unnamed x11, local copies, waits for them, and re-layouts  6.19 us

profile of v1, /device:TPU:25, one launch (start us, length us, event | category | flops | bytes accessed | tf_op | source)
XLA Modules:
  0.0 103.9 jit_solution(16482564284592936164)
XLA Ops:
  0.0 0.0 copy-start
  0.0 1.6 %copy-done = bf16[1,512,2048]{2,1,0:T(8,128)(2,1)S(1)} copy-done((bf16[1,512,2048]{2,1,0:T(8,128)(2,1)S(1)}, bf16[1,512,2048]{2,1,0:T(8,128)(2,1)}, u32[]{:S(2)}) %copy-start) | copy-done | bytes 2097176
  1.6 0.0 copy-start.1
  1.6 1.2 %copy-done.1 = bf16[2,512,512]{2,1,0:T(8,128)(2,1)S(1)} copy-done((bf16[2,512,512]{2,1,0:T(8,128)(2,1)S(1)}, bf16[2,512,512]{2,1,0:T(8,128)(2,1)}, u32[]{:S(2)}) %copy-start.1) | copy-done | bytes 1048600
  2.8 0.0 copy-start.2
  2.8 1.0 %copy-done.2 = bf16[1,512,512]{2,1,0:T(8,128)(2,1)S(1)} copy-done((bf16[1,512,512]{2,1,0:T(8,128)(2,1)S(1)}, bf16[1,512,512]{2,1,0:T(8,128)(2,1)}, u32[]{:S(2)}) %copy-start.2) | copy-done | bytes 524312
  3.9 0.0 copy-start.3
  3.9 0.7 copy-done.3
  4.5 0.0 copy-start.4
  4.5 0.7 copy-done.4
  5.2 97.7 %shard_map.55 = bf16[1,2,512,512]{3,2,1,0:T(8,128)(2,1)S(1)} custom-call(bf16[2,512,512]{2,1,0:T(8,128)(2,1)S(1)} %copy-done.1, bf16[1,512,2048]{2,1,0:T(8,128)(2,1)S(1)} %copy-done, bf16[1,512,512]{2,1,0:T(8,128)(2,1)S(1)} %copy-done.2, s32[2,16]{1,0:T(2,128)S(1)} %copy-done.3, s32[2,64]{1,0:T(2,128)S(1)} %copy-done.4), custom_call_target="tpu_custom_call" | custom-call | tf_op jit(solution)/shard_map/pallas_call | solution.py:191
  102.9 1.0 copy.7
Async XLA Ops:
  0.0 1.6 %copy-start = (bf16[1,512,2048]{2,1,0:T(8,128)(2,1)S(1)}, bf16[1,512,2048]{2,1,0:T(8,128)(2,1)}, u32[]{:S(2)}) copy-start(bf16[1,512,2048]{2,1,0:T(8,128)(2,1)} %win.1) | copy-start | bytes 6291460
  1.6 1.2 %copy-start.1 = (bf16[2,512,512]{2,1,0:T(8,128)(2,1)S(1)}, bf16[2,512,512]{2,1,0:T(8,128)(2,1)}, u32[]{:S(2)}) copy-start(bf16[2,512,512]{2,1,0:T(8,128)(2,1)} %inp.1) | copy-start | bytes 3145732
  2.8 1.0 %copy-start.2 = (bf16[1,512,512]{2,1,0:T(8,128)(2,1)S(1)}, bf16[1,512,512]{2,1,0:T(8,128)(2,1)}, u32[]{:S(2)}) copy-start(bf16[1,512,512]{2,1,0:T(8,128)(2,1)} %wout.1) | copy-start | bytes 1572868
  3.9 0.7 copy-start.3
  4.5 0.7 copy-start.4

commit v2 on v1

v2 whole, which is shorter than its diff:
```python
import functools
import math

import jax
import jax.numpy as jnp
from jax import lax
from jax.experimental import pallas as pl
from jax.experimental.pallas import tpu as pltpu
from jax.sharding import PartitionSpec as P

MESH = pl.DeviceIdType.MESH

HEAD_DIM = 128
WINDOW = 512
CH = 128
SUB = 64
HELPERS = (2, 6)
BF = jnp.bfloat16
F32 = jnp.float32

norm_eps = 1e-05
out_eps = 0.001


def half_silu(h):
    h = h.astype(BF)
    return h + h * jnp.tanh(h)


def centred(x, epsilon):
    mean = jnp.mean(x, axis=-1, keepdims=True)
    cen = x - mean
    return cen, lax.rsqrt(jnp.mean(cen * cen, axis=-1, keepdims=True) + epsilon)


def kernel(micro, tok, width, hd, sections, blocks, streams,
           inp, win, wout, lens_hbm, valid_hbm, out,
           ob, xin, hx, w1, w2, qb, ub, kb, vb, acc, mask, lens, valid,
           ld_sem, out_sem, xs, xr, hs, hr, fs, js):
    p = lax.axis_index("pipe")
    b = lax.axis_index("seq")
    heads = hd // HEAD_DIM
    span = WINDOW + CH
    n_ch = tok // CH
    n_sub = CH // SUB
    right = lax.rem(b + 1, blocks)
    left = lax.rem(b + blocks - 1, blocks)
    up = lax.rem(p + 1, sections)
    down = lax.rem(p + sections - 1, sections)
    even = lax.rem(p, 2) == 0
    last = p == sections - 1

    barrier = pltpu.get_barrier_semaphore()
    for dev in ((p, left), (p, right), (up, b), (down, b), (up, right), (down, left)):
        pl.semaphore_signal(barrier, inc=1, device_id=dev, device_id_type=MESH)

    @pl.when(p == 0)
    def _():
        for helper in HELPERS:
            pl.semaphore_signal(barrier, inc=1, device_id=(helper, left), device_id_type=MESH)

    load_x = pltpu.make_async_copy(inp, xin, ld_sem.at[0])
    load_in = pltpu.make_async_copy(win.at[0], w1, ld_sem.at[1])
    load_out = pltpu.make_async_copy(wout.at[0], w2, ld_sem.at[2])
    load_len = pltpu.make_async_copy(lens_hbm, lens, ld_sem.at[3])
    load_val = pltpu.make_async_copy(valid_hbm, valid, ld_sem.at[4])

    @pl.when(p == 0)
    def _():
        load_x.start()

    load_len.start()
    load_val.start()
    load_in.start()
    load_out.start()

    def sub_rows(k, j):
        return pl.ds(pl.multiple_of(k * CH + j * SUB, SUB), SUB)

    def x_copy(m, k, j):
        return pltpu.make_async_remote_copy(
            src_ref=ob.at[m, sub_rows(k, j)], dst_ref=xin.at[m, sub_rows(k, j)],
            send_sem=xs.at[m, k, j], recv_sem=xr.at[m, k, j],
            device_id=(up, b), device_id_type=MESH)

    def h_copy(m, k, j):
        return pltpu.make_async_remote_copy(
            src_ref=xin.at[m, sub_rows(k, j)], dst_ref=hx.at[m, sub_rows(k, j)],
            send_sem=hs.at[m, k, j], recv_sem=hr.at[m, k, j],
            device_id=(p, right), device_id_type=MESH)

    def i_copy(m, k, j):
        return pltpu.make_async_remote_copy(
            src_ref=inp.at[m, sub_rows(k, j)], dst_ref=hx.at[m, sub_rows(k, j)],
            send_sem=js.at[m, k, j], recv_sem=hr.at[m, k, j],
            device_id=(0, right), device_id_type=MESH)

    def f_copy(m, k, j):
        return pltpu.make_async_remote_copy(
            src_ref=ob.at[m, sub_rows(k, j)], dst_ref=hx.at[m, sub_rows(k, j)],
            send_sem=fs.at[m, k, j], recv_sem=hr.at[m, k, j],
            device_id=(up, right), device_id_type=MESH)

    def rows_of(k):
        return pl.ds(pl.multiple_of(k * CH, CH), CH)

    def out_copy(m, k):
        return pltpu.make_async_copy(
            ob.at[m, rows_of(k)], out.at[0, m, rows_of(k)], out_sem.at[m, k])

    first_sends = {0: [(0, 3), (0, 0)], HELPERS[0]: [(0, 2), (1, 3), (1, 1)],
                   HELPERS[1]: [(0, 1), (1, 2), (1, 0)]}
    helps = (p == HELPERS[0]) | (p == HELPERS[1])
    pl.semaphore_wait(barrier, jnp.where(helps, 7, 6))

    for sender, pieces in first_sends.items():
        @pl.when(p == sender)
        def _():
            for m, k in pieces:
                for j in range(n_sub):
                    i_copy(m, k, j).start()

    @pl.when(p == 0)
    def _():
        load_x.wait()

    load_len.wait()
    load_val.wait()

    score_scale = 0.5 / math.sqrt(HEAD_DIM)
    ii = lax.broadcasted_iota(jnp.int32, (CH, 1), 0)
    jj = lax.broadcasted_iota(jnp.int32, (1, span), 1)

    def make_mask(step, carry):
        m = step // n_ch
        k = lax.rem(step, n_ch)
        row = k * CH + ii
        col = k * CH + jj - WINDOW
        q_pos = b * tok + row
        k_pos = b * tok + col
        q_stream = jnp.zeros_like(q_pos)
        k_stream = jnp.zeros_like(k_pos)
        bound = jnp.int32(0)
        for n in range(streams):
            bound = bound + lens[m, n]
            q_stream = q_stream + jnp.where(q_pos >= bound, 1, 0)
            k_stream = k_stream + jnp.where(k_pos >= bound, 1, 0)
        here = valid[m, b]
        before = valid[m, left]
        k_count = jnp.where(col >= 0, here, before)
        k_row = jnp.where(col >= 0, col, col + tok)
        k_code = jnp.where((k_row < k_count) & (k_pos >= 0), k_stream, -1)
        q_code = jnp.where(row < here, q_stream, -2)
        ok = (q_code == k_code) & (jj > ii) & (jj <= ii + WINDOW)
        mask[m, k] = jnp.where(ok, score_scale, 0.0)
        return carry

    lax.fori_loop(0, micro * n_ch, make_mask, 0)
    load_in.wait()
    load_out.wait()

    def project(x, targets):
        cen, rstd = centred(x.astype(F32), norm_eps)
        cen = cen.astype(BF)
        for ref, at, rows in targets:
            ref[rows] = half_silu(jnp.dot(
                cen, w1[:, at * hd:(at + 1) * hd], preferred_element_type=F32) * (0.5 * rstd))

    def weigh(m, q, lo, hi):
        rows = slice(q * CH, (q + 1) * CH)
        keys = slice(lo * CH, hi * CH)
        mk = mask[m, q, :, (lo - q) * CH:(hi - q) * CH]
        raw = [lax.dot_general(qb[rows, c], kb[keys, c], (((1,), (1,)), ((), ())),
                               preferred_element_type=F32) for c in head_cols]
        return lo, hi, [half_silu(s * mk) for s in raw]

    def mix(weighed):
        lo, hi, weights = weighed
        keys = slice(lo * CH, hi * CH)
        return jnp.concatenate([jnp.dot(w, vb[keys, c], preferred_element_type=F32)
                                for w, c in zip(weights, head_cols)], 1)

    head_cols = [slice(h * HEAD_DIM, (h + 1) * HEAD_DIM) for h in range(heads)]
    lead = WINDOW // CH

    def chunk(k):
        return slice(k * CH, (k + 1) * CH)

    def gather_weights(m, j):
        return [(q, weigh(m, q, lead + j, lead + j + 1)) for q in range(j, n_ch)]

    def gather_mix(j, weighed):
        for q, w in weighed:
            acc[chunk(q)] = mix(w) if q == j else acc[chunk(q)] + mix(w)

    def own(m, k):
        @pl.when(p > 0)
        def _():
            for j in range(n_sub):
                x_copy(m, k, j).wait_recv()
                if k > 0:
                    @pl.when(even)
                    def _():
                        h_copy(m, k, j).start()

        weighed = gather_weights(m, k + 1) if 0 < k < n_ch - 1 else None
        at = chunk(lead + k)
        project(xin[m, chunk(k)],
                ((kb, 3, at), (vb, 1, at), (qb, 2, chunk(k)), (ub, 0, chunk(k))))
        if weighed:
            gather_mix(k + 1, weighed)

    def attend(m, k):
        rows = chunk(k)
        for j in range(n_sub):
            h_copy(m, k, j).wait_recv()
        ahead = weigh(m, k - 1, k + 1, lead + 1) if k > 0 else None
        close = weigh(m, k, lead, lead + 1) if k == n_ch - 1 else None
        project(hx[m, rows], ((kb, 3, rows), (vb, 1, rows)))
        att = acc[rows]
        if close:
            att = att + mix(close)
        if ahead:
            got = mix(ahead)
        tail = weigh(m, k, k, k + 1)
        if ahead:
            more = weigh(m, k - 1, k, k + 1)
        att = att + mix(tail)
        if ahead:
            got = got + mix(more)
            acc[chunk(k - 1)] = got if k == 1 else acc[chunk(k - 1)] + got
        cen, rstd = centred(att, out_eps * WINDOW)
        gated = (cen * ub[rows].astype(F32)).astype(BF)
        res = xin[m, rows].astype(F32) + rstd * jnp.dot(
            gated, w2[...], preferred_element_type=F32)
        ob[m, rows] = res.astype(BF)
        out_copy(m, k).start()

        @pl.when(jnp.logical_not(last))
        def _():
            for j in range(n_sub):
                x_copy(m, k, j).start()

        @pl.when(jnp.logical_not(last) if k == 0 else even)
        def _():
            for j in range(n_sub):
                f_copy(m, k, j).start()

    def layer(m, carry):
        for k in range(n_ch - 1, -1, -1):
            if k == 0:
                gather_mix(1, gather_weights(m, 1))
            own(m, k)
        for k in range(n_ch - 1, -1, -1):
            attend(m, k)
        return carry

    lax.fori_loop(0, micro, layer, 0)

    for sender, pieces in first_sends.items():
        @pl.when(p == sender)
        def _():
            for m, k in pieces:
                for j in range(n_sub):
                    i_copy(m, k, j).wait_send()

    for m in range(micro):
        for k in range(n_ch):
            out_copy(m, k).wait()

    for m in range(micro):
        for k in range(n_ch):
            for j in range(n_sub):
                if k > 0:
                    @pl.when(even & (p > 0))
                    def _():
                        h_copy(m, k, j).wait_send()

                @pl.when(jnp.logical_not(last) if k == 0 else even)
                def _():
                    f_copy(m, k, j).wait_send()

    @pl.when(jnp.logical_not(last))
    def _():
        for m in range(micro):
            for k in range(n_ch):
                for j in range(n_sub):
                    x_copy(m, k, j).wait_send()


def shards(mesh, inputs, w_in, w_out, lengths, valid):
    micro, tok, width = inputs.shape
    hd = w_out.shape[1]
    sections = mesh.shape["pipe"]
    blocks = mesh.shape["seq"]
    streams = lengths.shape[1]
    n_ch = tok // CH
    hbm = pl.BlockSpec(memory_space=pltpu.HBM)
    return pl.pallas_call(
        functools.partial(kernel, micro, tok, width, hd, sections, blocks, streams),
        out_shape=jax.ShapeDtypeStruct((1, micro, tok, width), BF),
        in_specs=[hbm] * 5,
        out_specs=hbm,
        scratch_shapes=[
            pltpu.VMEM((micro, tok, width), BF),
            pltpu.VMEM((micro, tok, width), BF),
            pltpu.VMEM((micro, tok, width), BF),
            pltpu.VMEM((width, 4 * hd), BF),
            pltpu.VMEM((hd, width), BF),
            pltpu.VMEM((tok, hd), BF),
            pltpu.VMEM((tok, hd), BF),
            pltpu.VMEM((WINDOW + tok, hd), BF),
            pltpu.VMEM((WINDOW + tok, hd), BF),
            pltpu.VMEM((tok, hd), F32),
            pltpu.VMEM((micro, n_ch, CH, WINDOW + CH), F32),
            pltpu.SMEM(lengths.shape, jnp.int32),
            pltpu.SMEM(valid.shape, jnp.int32),
            pltpu.SemaphoreType.DMA((5,)),
            pltpu.SemaphoreType.DMA((micro, n_ch)),
        ] + [pltpu.SemaphoreType.DMA((micro, n_ch, CH // SUB))] * 6,
        compiler_params=pltpu.CompilerParams(
            collective_id=0, has_side_effects=True, vmem_limit_bytes=67043328),
    )(inputs, w_in, w_out, lengths, valid)


def solution(mesh):
    in_specs = (P(None, "seq", None), P("pipe", None, None), P("pipe", None, None), P(), P())
    out_specs = P("pipe", None, "seq", None)
    return jax.shard_map(functools.partial(shards, mesh), mesh=mesh, in_specs=in_specs,
                         out_specs=out_specs, check_vma=False)
```

time: 104 us -> 95 us (0.913)
  Pallas kernels: 97.7 us -> 92.6 us
  local copies, waits for them, and re-layouts: 6.19 us -> 2.26 us
    pallas_call x1, Pallas kernels: 97.7 us -> 92.6 us  [shards(): pl.pallas_call(functools.partial(kernel, micro, tok, width, hd, sections,...]
    unnamed x11 -> x1, local copies, waits for them, and re-layouts: 6.19 us -> 2.26 us
where the time goes in v2:
time: 95 us; the launch traced here: 94.8 us
  Pallas kernels  92.6 us (97%)
  local copies, waits for them, and re-layouts  2.26 us (2%)
    pallas_call x1, Pallas kernels, shards(): pl.pallas_call(functools.partial(kernel, micro, tok, width, hd, sections,...  92.6 us
    unnamed x1, local copies, waits for them, and re-layouts  2.26 us

profile of v2, /device:TPU:25, one launch (start us, length us, event | category | flops | bytes accessed | tf_op | source)
XLA Modules:
  0.0 94.8 jit_solution(10146980900282975420)
XLA Ops:
  0.0 92.6 %shard_map.55 = bf16[1,2,512,512]{3,2,1,0:T(8,128)(2,1)} custom-call(bf16[2,512,512]{2,1,0:T(8,128)(2,1)} %inp.1, bf16[1,512,2048]{2,1,0:T(8,128)(2,1)} %win.1, bf16[1,512,512]{2,1,0:T(8,128)(2,1)} %wout.1, s32[2,16]{1,0:T(2,128)} %lens_hbm.1, s32[2,64]{1,0:T(2,128)} %valid_hbm.1), custom_call_target="tpu_custom_call" | custom-call | tf_op jit(solution)/shard_map/pallas_call | solution.py:299
  92.6 2.3 %copy.7 = bf16[1,2,512,512]{3,2,1,0:T(8,128)(2,1)} copy(bf16[1,2,512,512]{3,2,1,0:T(8,128)(2,1)} %shard_map.55) | data formatting | bytes 2097152

commit v3 on v2

--- a/solution.py
+++ b/solution.py
@@ -35,8 +35,8 @@
 
 def kernel(micro, tok, width, hd, sections, blocks, streams,
            inp, win, wout, lens_hbm, valid_hbm, out,
-           ob, xin, hx, w1, w2, qb, ub, kb, vb, acc, mask, lens, valid,
-           ld_sem, out_sem, xs, xr, hs, hr, fs, js):
+           ib, ob, xin, hx, w1, w2, qb, ub, kb, vb, acc, mask, lens, valid,
+           ld_sem, ib_sem, out_sem, xs, xr, hs, hr, fs, js):
     p = lax.axis_index("pipe")
     b = lax.axis_index("seq")
     heads = hd // HEAD_DIM
@@ -59,6 +59,14 @@
         for helper in HELPERS:
             pl.semaphore_signal(barrier, inc=1, device_id=(helper, left), device_id_type=MESH)
 
+    first_sends = {0: [(0, 3), (0, 1)], HELPERS[0]: [(0, 2), (1, 3), (1, 1)],
+                   HELPERS[1]: [(0, 0), (1, 2), (1, 0)]}
+
+    def first_load(pieces, n):
+        m, k = pieces[n]
+        return pltpu.make_async_copy(
+            inp.at[m, k * CH:(k + 1) * CH], ib.at[n * CH:(n + 1) * CH], ib_sem.at[n])
+
     load_x = pltpu.make_async_copy(inp, xin, ld_sem.at[0])
     load_in = pltpu.make_async_copy(win.at[0], w1, ld_sem.at[1])
     load_out = pltpu.make_async_copy(wout.at[0], w2, ld_sem.at[2])
@@ -69,6 +77,12 @@
     def _():
         load_x.start()
 
+    for sender, pieces in first_sends.items():
+        @pl.when(p == sender)
+        def _():
+            for n in range(len(pieces)):
+                first_load(pieces, n).start()
+
     load_len.start()
     load_val.start()
     load_in.start()
@@ -89,9 +103,9 @@
             send_sem=hs.at[m, k, j], recv_sem=hr.at[m, k, j],
             device_id=(p, right), device_id_type=MESH)
 
-    def i_copy(m, k, j):
+    def i_copy(m, k, j, n):
         return pltpu.make_async_remote_copy(
-            src_ref=inp.at[m, sub_rows(k, j)], dst_ref=hx.at[m, sub_rows(k, j)],
+            src_ref=ib.at[sub_rows(n, j)], dst_ref=hx.at[m, sub_rows(k, j)],
             send_sem=js.at[m, k, j], recv_sem=hr.at[m, k, j],
             device_id=(0, right), device_id_type=MESH)
 
@@ -108,17 +122,21 @@
         return pltpu.make_async_copy(
             ob.at[m, rows_of(k)], out.at[0, m, rows_of(k)], out_sem.at[m, k])
 
-    first_sends = {0: [(0, 3), (0, 0)], HELPERS[0]: [(0, 2), (1, 3), (1, 1)],
-                   HELPERS[1]: [(0, 1), (1, 2), (1, 0)]}
+    for sender, pieces in first_sends.items():
+        @pl.when(p == sender)
+        def _():
+            for n in range(len(pieces)):
+                first_load(pieces, n).wait()
+
     helps = (p == HELPERS[0]) | (p == HELPERS[1])
     pl.semaphore_wait(barrier, jnp.where(helps, 7, 6))
 
     for sender, pieces in first_sends.items():
         @pl.when(p == sender)
         def _():
-            for m, k in pieces:
+            for n, (m, k) in enumerate(pieces):
                 for j in range(n_sub):
-                    i_copy(m, k, j).start()
+                    i_copy(m, k, j, n).start()
 
     @pl.when(p == 0)
     def _():
@@ -198,10 +216,10 @@
         def _():
             for j in range(n_sub):
                 x_copy(m, k, j).wait_recv()
-                if k > 0:
-                    @pl.when(even)
-                    def _():
-                        h_copy(m, k, j).start()
+
+                @pl.when(even)
+                def _():
+                    h_copy(m, k, j).start()
 
         weighed = gather_weights(m, k + 1) if 0 < k < n_ch - 1 else None
         at = chunk(lead + k)
@@ -210,24 +228,31 @@
         if weighed:
             gather_mix(k + 1, weighed)
 
+    def halo(m, k):
+        for j in range(n_sub):
+            h_copy(m, k, j).wait_recv()
+
     def attend(m, k):
         rows = chunk(k)
-        for j in range(n_sub):
-            h_copy(m, k, j).wait_recv()
-        ahead = weigh(m, k - 1, k + 1, lead + 1) if k > 0 else None
-        close = weigh(m, k, lead, lead + 1) if k == n_ch - 1 else None
-        project(hx[m, rows], ((kb, 3, rows), (vb, 1, rows)))
-        att = acc[rows]
-        if close:
-            att = att + mix(close)
-        if ahead:
-            got = mix(ahead)
-        tail = weigh(m, k, k, k + 1)
-        if ahead:
-            more = weigh(m, k - 1, k, k + 1)
-        att = att + mix(tail)
-        if ahead:
-            got = got + mix(more)
+        if k == n_ch - 1:
+            tail = weigh(m, k, k, lead + 1)
+            more = weigh(m, k - 1, k, lead + 1)
+            att = acc[rows] + mix(tail)
+            got = mix(more)
+        else:
+            halo(m, k)
+            ahead = weigh(m, k - 1, k + 1, lead + 1) if k > 0 else None
+            project(hx[m, rows], ((kb, 3, rows), (vb, 1, rows)))
+            att = acc[rows]
+            if ahead:
+                got = mix(ahead)
+            tail = weigh(m, k, k, k + 1)
+            if ahead:
+                more = weigh(m, k - 1, k, k + 1)
+            att = att + mix(tail)
+            if ahead:
+                got = got + mix(more)
+        if k > 0:
             acc[chunk(k - 1)] = got if k == 1 else acc[chunk(k - 1)] + got
         cen, rstd = centred(att, out_eps * WINDOW)
         gated = (cen * ub[rows].astype(F32)).astype(BF)
@@ -241,7 +266,7 @@
             for j in range(n_sub):
                 x_copy(m, k, j).start()
 
-        @pl.when(jnp.logical_not(last) if k == 0 else even)
+        @pl.when(even)
         def _():
             for j in range(n_sub):
                 f_copy(m, k, j).start()
@@ -250,6 +275,9 @@
         for k in range(n_ch - 1, -1, -1):
             if k == 0:
                 gather_mix(1, gather_weights(m, 1))
+                halo(m, n_ch - 1)
+                top = chunk(n_ch - 1)
+                project(hx[m, top], ((kb, 3, top), (vb, 1, top)))
             own(m, k)
         for k in range(n_ch - 1, -1, -1):
             attend(m, k)
@@ -260,9 +288,9 @@
     for sender, pieces in first_sends.items():
         @pl.when(p == sender)
         def _():
-            for m, k in pieces:
+            for n, (m, k) in enumerate(pieces):
                 for j in range(n_sub):
-                    i_copy(m, k, j).wait_send()
+                    i_copy(m, k, j, n).wait_send()
 
     for m in range(micro):
         for k in range(n_ch):
@@ -271,12 +299,11 @@
     for m in range(micro):
         for k in range(n_ch):
             for j in range(n_sub):
-                if k > 0:
-                    @pl.when(even & (p > 0))
-                    def _():
-                        h_copy(m, k, j).wait_send()
-
-                @pl.when(jnp.logical_not(last) if k == 0 else even)
+                @pl.when(even & (p > 0))
+                def _():
+                    h_copy(m, k, j).wait_send()
+
+                @pl.when(even)
                 def _():
                     f_copy(m, k, j).wait_send()
 
@@ -302,6 +329,7 @@
         in_specs=[hbm] * 5,
         out_specs=hbm,
         scratch_shapes=[
+            pltpu.VMEM((3 * CH, width), BF),
             pltpu.VMEM((micro, tok, width), BF),
             pltpu.VMEM((micro, tok, width), BF),
             pltpu.VMEM((micro, tok, width), BF),
@@ -316,6 +344,7 @@
             pltpu.SMEM(lengths.shape, jnp.int32),
             pltpu.SMEM(valid.shape, jnp.int32),
             pltpu.SemaphoreType.DMA((5,)),
+            pltpu.SemaphoreType.DMA((3,)),
             pltpu.SemaphoreType.DMA((micro, n_ch)),
         ] + [pltpu.SemaphoreType.DMA((micro, n_ch, CH // SUB))] * 6,
         compiler_params=pltpu.CompilerParams(

time: 95 us -> 89 us (0.937)
  Pallas kernels: 92.6 us -> 86.6 us
    pallas_call x1, Pallas kernels: 92.6 us -> 86.6 us  [shards(): pl.pallas_call(functools.partial(kernel, micro, tok, width, hd, sections,...]
where the time goes in v3:
time: 89 us; the launch traced here: 88.8 us
  Pallas kernels  86.6 us (97%)
  local copies, waits for them, and re-layouts  2.26 us (3%)
    pallas_call x1, Pallas kernels, shards(): pl.pallas_call(functools.partial(kernel, micro, tok, width, hd, sections,...  86.6 us
    unnamed x1, local copies, waits for them, and re-layouts  2.26 us

profile of v3, /device:TPU:25, one launch (start us, length us, event | category | flops | bytes accessed | tf_op | source)
XLA Modules:
  0.0 88.8 jit_solution(9730875703343784966)
XLA Ops:
  0.0 86.6 %shard_map.55 = bf16[1,2,512,512]{3,2,1,0:T(8,128)(2,1)} custom-call(bf16[2,512,512]{2,1,0:T(8,128)(2,1)} %inp.1, bf16[1,512,2048]{2,1,0:T(8,128)(2,1)} %win.1, bf16[1,512,512]{2,1,0:T(8,128)(2,1)} %wout.1, s32[2,16]{1,0:T(2,128)} %lens_hbm.1, s32[2,64]{1,0:T(2,128)} %valid_hbm.1), custom_call_target="tpu_custom_call" | custom-call | tf_op jit(solution)/shard_map/pallas_call | solution.py:326
  86.6 2.3 %copy.7 = bf16[1,2,512,512]{3,2,1,0:T(8,128)(2,1)} copy(bf16[1,2,512,512]{3,2,1,0:T(8,128)(2,1)} %shard_map.55) | data formatting | bytes 2097152

commit v4 on v3

--- a/solution.py
+++ b/solution.py
@@ -173,13 +173,19 @@
         mask[m, k] = jnp.where(ok, score_scale, 0.0)
         return carry
 
-    lax.fori_loop(0, micro * n_ch, make_mask, 0)
+    lax.fori_loop(0, jnp.where(p == 0, n_ch, micro * n_ch), make_mask, 0)
     load_in.wait()
     load_out.wait()
 
+    def prepare(x):
+        cen, rstd = centred(x.astype(F32), norm_eps)
+        return cen.astype(BF), rstd
+
     def project(x, targets):
-        cen, rstd = centred(x.astype(F32), norm_eps)
-        cen = cen.astype(BF)
+        project_from(prepare(x), targets)
+
+    def project_from(prepared, targets):
+        cen, rstd = prepared
         for ref, at, rows in targets:
             ref[rows] = half_silu(jnp.dot(
                 cen, w1[:, at * hd:(at + 1) * hd], preferred_element_type=F32) * (0.5 * rstd))
@@ -223,22 +229,27 @@
 
         weighed = gather_weights(m, k + 1) if 0 < k < n_ch - 1 else None
         at = chunk(lead + k)
-        project(xin[m, chunk(k)],
-                ((kb, 3, at), (vb, 1, at), (qb, 2, chunk(k)), (ub, 0, chunk(k))))
+        prepared = prepare(xin[m, chunk(k)])
+        project_from(prepared, ((kb, 3, at), (vb, 1, at)))
+        later = (qb, 2, chunk(k)), (ub, 0, chunk(k))
+        if k > 0:
+            project_from(prepared, later)
         if weighed:
             gather_mix(k + 1, weighed)
+        return prepared, later
 
     def halo(m, k):
         for j in range(n_sub):
             h_copy(m, k, j).wait_recv()
 
-    def attend(m, k):
+    def attend(m, k, pending):
         rows = chunk(k)
         if k == n_ch - 1:
             tail = weigh(m, k, k, lead + 1)
             more = weigh(m, k - 1, k, lead + 1)
             att = acc[rows] + mix(tail)
             got = mix(more)
+            project_from(*pending)
         else:
             halo(m, k)
             ahead = weigh(m, k - 1, k + 1, lead + 1) if k > 0 else None
@@ -272,15 +283,19 @@
                 f_copy(m, k, j).start()
 
     def layer(m, carry):
+        @pl.when((p == 0) & (m > 0))
+        def _():
+            lax.fori_loop(m * n_ch, (m + 1) * n_ch, make_mask, 0)
+
         for k in range(n_ch - 1, -1, -1):
             if k == 0:
                 gather_mix(1, gather_weights(m, 1))
                 halo(m, n_ch - 1)
                 top = chunk(n_ch - 1)
                 project(hx[m, top], ((kb, 3, top), (vb, 1, top)))
-            own(m, k)
+            pending = own(m, k)
         for k in range(n_ch - 1, -1, -1):
-            attend(m, k)
+            attend(m, k, pending)
         return carry
 
     lax.fori_loop(0, micro, layer, 0)

time: 89 us -> 88.8 us (level)
  no operation moved by 1% of the time
where the time goes in v4:
time: 88.8 us; the launch traced here: 88.7 us
  Pallas kernels  86.4 us (97%)
  local copies, waits for them, and re-layouts  2.26 us (3%)
    pallas_call x1, Pallas kernels, shards(): pl.pallas_call(functools.partial(kernel, micro, tok, width, hd, sections,...  86.4 us
    unnamed x1, local copies, waits for them, and re-layouts  2.26 us

profile of v4, /device:TPU:25, one launch (start us, length us, event | category | flops | bytes accessed | tf_op | source)
XLA Modules:
  0.0 88.7 jit_solution(7633636693593523750)
XLA Ops:
  0.0 86.4 %shard_map.55 = bf16[1,2,512,512]{3,2,1,0:T(8,128)(2,1)} custom-call(bf16[2,512,512]{2,1,0:T(8,128)(2,1)} %inp.1, bf16[1,512,2048]{2,1,0:T(8,128)(2,1)} %win.1, bf16[1,512,512]{2,1,0:T(8,128)(2,1)} %wout.1, s32[2,16]{1,0:T(2,128)} %lens_hbm.1, s32[2,64]{1,0:T(2,128)} %valid_hbm.1), custom_call_target="tpu_custom_call" | custom-call | tf_op jit(solution)/shard_map/pallas_call | solution.py:341
  86.4 2.3 %copy.7 = bf16[1,2,512,512]{3,2,1,0:T(8,128)(2,1)} copy(bf16[1,2,512,512]{3,2,1,0:T(8,128)(2,1)} %shard_map.55) | data formatting | bytes 2097152
